TPU v7x, 32 devices: a whole 2x2x4 slice. The times are simulated.
32 devices in a mesh: fsdp: 4 (over x, core), tm: 8 (over z, y).
Axes of the slice: x: 2, y: 2, z: 4, core: 2. Of those that a mesh axis runs over, the one named last changes fastest.
Arguments:
- tokens: bfloat16 [8, 8, 256, 1024], P('fsdp', 'tm'), may hold values from -6 to 6
- spatial_gain: float32 [1024], replicated, may hold values from 0.25 to 1.75
- spatial_qkv: bfloat16 [1024, 1536], P('fsdp'), may hold values from -16 to 16
- spatial_out: bfloat16 [512, 1024], P('fsdp'), may hold values from -0.25 to 0.25
- temporal_gain: float32 [1024], replicated, may hold values from 0.25 to 1.75
- temporal_qkv: bfloat16 [1024, 1536], P('fsdp'), may hold values from -16 to 16
- temporal_out: bfloat16 [512, 1024], P('fsdp'), may hold values from -0.25 to 0.25
Outputs:
- encoded: bfloat16 [8, 8, 256, 1024], P('fsdp', 'tm')
All inputs are finite; a program needn't handle non-finite values.
Results may differ from a plain program's by a relative error of at most 0.0061.
Values may be sent and summed in bfloat16 or wider, within the bound.
A program may use at most 64 MiB of HBM per device.

v0:
```python
import jax
import jax.numpy as jnp
from jax import lax
from jax.sharding import PartitionSpec as P

HEAD = 64
HEADS = 8
INNER = 512


EPSILON = 1e-06


def norm_rows(source, norm_gain):
    values = source.astype(jnp.float32)
    centre = values - jnp.mean(values, axis=-1, keepdims=True)
    spread = jnp.mean(centre * centre, axis=-1, keepdims=True)
    return (centre * lax.rsqrt(spread + EPSILON) * norm_gain).astype(jnp.bfloat16)


def attention_core(projected):
    inner_width = projected.shape[-1] // 3
    lead_shape = projected.shape[:-1]
    queries = projected[..., :inner_width].reshape(lead_shape + (HEADS, HEAD))
    key_rows = projected[..., inner_width : 2 * inner_width].reshape(lead_shape + (HEADS, HEAD))
    value_rows = (
        projected[..., 2 * inner_width :].astype(jnp.bfloat16).reshape(lead_shape + (HEADS, HEAD))
    )
    scores = jnp.einsum(
        "blmhe,bkmhe->bmhlk", queries, key_rows, precision=lax.Precision.HIGHEST
    ) * HEAD ** (-0.5)
    row_max = jnp.max(scores, axis=-1, keepdims=True)
    exponent = jnp.exp(scores - row_max)
    weights = (exponent / jnp.sum(exponent, axis=-1, keepdims=True)).astype(jnp.bfloat16)
    context = jnp.einsum(
        "bmhlk,bkmhe->blmhe", weights, value_rows, preferred_element_type=jnp.float32
    )
    return context.astype(jnp.bfloat16).reshape(lead_shape + (inner_width,))


def project_inputs(normed, weight):

    def add_rows(running, segment, offset):
        return jnp.dot(normed, segment, preferred_element_type=jnp.float32)

    initial = jnp.zeros((normed.shape[0], weight.shape[1]), jnp.float32)
    return add_rows(initial, lax.all_gather(weight, "fsdp", axis=0, tiled=True), jnp.int32(0))


def project_outputs(context, weight):

    def add_rows(running, segment, offset):
        return jnp.dot(context, segment, preferred_element_type=jnp.float32)

    initial = jnp.zeros((context.shape[0], weight.shape[1]), jnp.float32)
    return add_rows(initial, lax.all_gather(weight, "fsdp", axis=0, tiled=True), jnp.int32(0))


def shards(
    tokens, spatial_gain, spatial_qkv, spatial_out, temporal_gain, temporal_qkv, temporal_out
):
    clip_count, frames, places, feature_width = tokens.shape
    row_count = clip_count * frames * places
    normed = norm_rows(tokens, spatial_gain).reshape(row_count, feature_width)
    projected = project_inputs(normed, spatial_qkv).reshape(
        clip_count * frames, places, 1, 3 * INNER
    )
    context = attention_core(projected).reshape(row_count, INNER)
    middle = (
        tokens.reshape(row_count, feature_width).astype(jnp.float32)
        + project_outputs(context, spatial_out)
    ).astype(jnp.bfloat16)
    middle = middle.reshape(clip_count, frames, places, feature_width)
    arrived = lax.all_to_all(middle, "tm", split_axis=2, concat_axis=1, tiled=True)
    full_frames = arrived.shape[1]
    few_places = arrived.shape[2]
    normed_t = norm_rows(arrived, temporal_gain).reshape(row_count, feature_width)
    projected_t = project_inputs(normed_t, temporal_qkv).reshape(
        clip_count, full_frames, few_places, 3 * INNER
    )
    context_t = attention_core(projected_t)
    returned_ctx = lax.all_to_all(context_t, "tm", split_axis=1, concat_axis=2, tiled=True)
    finished = middle.reshape(row_count, feature_width).astype(jnp.float32) + project_outputs(
        returned_ctx.reshape(row_count, INNER), temporal_out
    )
    return finished.astype(jnp.bfloat16).reshape(clip_count, frames, places, feature_width)


def solution(mesh):
    placed = (
        P("fsdp", "tm", None, None),
        P(),
        P("fsdp", None),
        P("fsdp", None),
        P(),
        P("fsdp", None),
        P("fsdp", None),
    )
    return jax.shard_map(
        shards, mesh=mesh, in_specs=placed, out_specs=P("fsdp", "tm", None, None), check_vma=False
    )
```

profile of v0, /device:TPU:0, one launch (start us, length us, event | category | flops | bytes accessed | tf_op | source)
XLA Modules:
  0.0 167.2 jit_solution(3869164747820133010)
XLA Ops:
  6.5 0.0 copy-start
  6.5 0.0 copy-start.5
  6.5 0.0 all-gather.5.cloned.1.call-start
  6.5 0.7 all-gather.5.cloned.1.call-update
  7.3 0.0 all-gather.7.cloned.1.call-start
  7.3 0.7 all-gather.7.cloned.1.call-update
  8.0 0.0 all-gather.9.cloned.1.call-start
  8.1 0.7 all-gather.9.cloned.1.call-update
  8.7 0.0 copy-done
  8.8 0.2 convert_reduce_fusion
  9.0 0.4 multiply_reduce_fusion.2
  9.4 30.8 %all-gather.5.cloned.1.call-done = bf16[1024,1536]{1,0:T(8,128)(2,1)} async-done(((bf16[256,1536]{1,0:T(8,128)(2,1)}), bf16[1024,1536]{1,0:T(8,128)(2,1)}) %all-gather.5.cloned.1.call-update) | async-done | bytes 3145744 | tf_op jit(solution)/shard_map/all_gather | solution.py:47
  40.2 0.0 copy-done.5
  40.2 3.8 %convolution_bitcast_fusion = f32[2,256,1,1536]{3,1,0,2:T(8,128)S(1)} fusion(bf16[1024,1536]{1,0:T(8,128)(2,1)} %all-gather.5.cloned.1.call-done, bf16[2,1,256,1024]{3,2,1,0:T(8,128)(2,1)S(1)} %copy-done, f32[1024]{0:T(1024)S(1)} %copy-done.5, f32[2,256]{1,0:T(2,128)S(1)} %add_rsqrt_fusion.1, f32[2,256]{1,0:T(2,128)S(1)} %broadcast_multiply_fusion.1), kind=kOutput, calls=%fused_computation.6 | convolution fusion | flops 1613234176 | bytes 7348224 | tf_op jit(solution)/shard_map/dot_general | solution.py:44
  44.0 0.0 copy-start.1
  44.0 1.7 %copy-done.1 = f32[2,256,1,1536]{3,1,0,2:T(8,128)} copy-done((f32[2,256,1,1536]{3,1,0,2:T(8,128)}, f32[2,256,1,1536]{3,1,0,2:T(8,128)S(1)}, u32[]{:S(2)}) %copy-start.1) | copy-done | bytes 3145752
  45.6 0.1 slice.35
  45.7 1.0 copy.81
  46.7 2.8 %fusion.36 = (f32[2,256,1,512]{3,1,0,2:T(8,128)S(1)}, f32[2,256,1,512]{3,1,0,2:T(8,128)}) fusion(f32[2,256,1,1536]{3,1,0,2:T(8,128)} %copy-done.1), kind=kLoop, calls=%fused_computation.54 | loop fusion | bytes 4194304 | tf_op jit(solution)/shard_map/slice | solution.py:25
  49.5 1.6 copy.82
  51.1 1.3 copy.83
  52.4 4.7 %fusion.39 = f32[2,8,256,256]{2,3,1,0:T(8,128)S(1)} fusion(f32[2,256,8,64]{1,3,2,0:T(8,128)S(1)} %bitcast.58, f32[2,256,8,64]{1,3,2,0:T(8,128)} %bitcast.59), kind=kOutput, calls=%fused_computation.57 | convolution fusion | flops 805306368 | bytes 6291456 | tf_op jit(solution)/shard_map/blmhe,bkmhe->bmhlk/dot_general | solution.py:29
  57.2 0.0 copy-start.4
  57.2 3.2 %fusion.37 = (f32[2,8,256]{2,1,0:T(8,128)S(1)}, f32[2,8,256,256]{2,3,1,0:T(8,128)S(1)}) fusion(f32[2,8,256,256]{2,3,1,0:T(8,128)S(1)} %fusion.39), kind=kOutput, calls=%fused_computation.55 | output fusion | flops 4194559 | bytes 8404992 | tf_op jit(solution)/shard_map/sub | solution.py:33
  60.4 0.0 copy-done.4
  60.4 0.5 fusion.20
  60.9 0.5 copy.85
  61.5 0.1 copy.104
  61.6 0.0 all-gather.7.cloned.1.call-done
  61.6 2.0 %fusion.8 = bf16[512,1024]{1,0:T(8,128)(2,1)S(1)} fusion(bf16[2,1,256,1024]{3,2,1,0:T(8,128)(2,1)S(1)} %copy-done, bf16[512,512]{0,1:T(8,128)(2,1)S(1)} %bitcast.65, bf16[512,1024]{1,0:T(8,128)(2,1)} %all-gather.7.cloned.1.call-done), kind=kOutput, calls=%fused_computation.11 | convolution fusion | flops 538443776 | bytes 3670016 | tf_op jit(solution)/shard_map/dot_general | solution.py:53
  63.6 0.0 copy-start.2
  63.6 1.0 copy-done.2
  64.5 2.0 %copy.86 = bf16[2,1,256,1024]{3,0,1,2:T(2,128)(2,1)} copy(bf16[2,1,256,1024]{3,2,0,1:T(8,128)(2,1)S(1)} %bitcast.62) | data formatting | bytes 2097152 | tf_op jit(solution)/shard_map/reshape | solution.py:73
  66.6 5.5 %all-to-all-start = ((bf16[2,1,256,1024]{3,0,1,2:T(2,128)(2,1)}), bf16[2,1,256,1024]{3,0,1,2:T(2,128)(2,1)S(1)}, u32[]{:S(2)}, u32[]{:S(2)}) async-start(bf16[2,1,256,1024]{3,0,1,2:T(2,128)(2,1)} %copy.86), calls=%async_computation | async-start | bytes 2097152 | tf_op jit(solution)/shard_map/all_to_all | solution.py:74
  72.1 0.0 all-gather.11.cloned.1.call-start
  72.1 0.5 all-gather.11.cloned.1.call-update
  72.6 25.6 %all-to-all-done = bf16[2,1,256,1024]{3,0,1,2:T(2,128)(2,1)S(1)} async-done(((bf16[2,1,256,1024]{3,0,1,2:T(2,128)(2,1)}), bf16[2,1,256,1024]{3,0,1,2:T(2,128)(2,1)S(1)}, u32[]{:S(2)}, u32[]{:S(2)}) %all-to-all-start) | async-done | bytes 1048608 | tf_op jit(solution)/shard_map/all_to_all | solution.py:74
  98.3 0.7 convert.12
  99.0 0.0 copy-start.6
  99.0 0.9 convert_reduce_fusion.1
  99.9 2.0 %multiply_reduce_fusion.1 = f32[2,256]{0,1:T(8,128)S(1)} fusion(bf16[2,1,256,1024]{3,0,1,2:T(2,128)(2,1)S(1)} %all-to-all-done, f32[2,256]{0,1:T(8,128)S(1)} %broadcast_multiply_fusion), kind=kLoop, calls=%fused_computation.22 | loop fusion | flops 2096640 | bytes 1052672 | tf_op jit(solution)/shard_map/reduce_sum | solution.py:17
  102.0 0.1 copy.121
  102.1 0.1 copy.122
  102.2 0.0 all-gather.9.cloned.1.call-done
  102.2 0.0 copy-done.6
  102.2 4.0 %fusion.5 = f32[2,8,32,1536]{3,2,1,0:T(8,128)S(1)} fusion(bf16[1024,1536]{1,0:T(8,128)(2,1)} %all-gather.9.cloned.1.call-done, f32[2,8,32,1024]{3,0,2,1:T(2,128)S(1)} %convert.12, f32[1024]{0:T(1024)S(1)} %copy-done.6, f32[2,8,32]{2,1,0:T(8,128)S(1)} %copy.121, f32[2,8,32]{2,1,0:T(8,128)S(1)} %copy.122), kind=kOutput, calls=%fused_computation.7 | convolution fusion | flops 1612709888 | bytes 8396800 | tf_op jit(solution)/shard_map/dot_general | solution.py:44
  106.2 1.1 fusion.35
  107.4 0.9 slice.34
  108.2 1.6 reshape.157
  109.8 1.8 %reshape.156 = f32[2,8,32,8,64]{4,3,2,1,0:T(8,128)} reshape(f32[2,8,32,512]{3,2,1,0:T(8,128)S(1)} %get-tuple-element.5) | data formatting | bytes 2097152 | tf_op jit(solution)/shard_map/reshape | solution.py:24
  111.6 1.6 reshape.155
  113.2 7.9 %fusion.9 = f32[2,32,8,8,8]{3,4,2,1,0:T(8,128)S(1)} fusion(f32[2,8,32,8,64]{4,3,2,1,0:T(8,128)S(1)} %reshape.157, f32[2,8,32,8,64]{4,3,2,1,0:T(8,128)} %reshape.156), kind=kOutput, calls=%fused_computation.12 | convolution fusion | flops 25165824 | bytes 2228224 | tf_op jit(solution)/shard_map/blmhe,bkmhe->bmhlk/dot_general | solution.py:29
  121.1 16.6 %fusion.38 = (f32[2,32,8,8]{3,2,1,0:T(8,128)S(1)}, f32[2,32,8,8,8]{3,4,2,1,0:T(8,128)S(1)}) fusion(f32[2,32,8,8,8]{3,4,2,1,0:T(8,128)S(1)} %fusion.9), kind=kOutput, calls=%fused_computation.56 | output fusion | flops 98311 | bytes 278528 | tf_op jit(solution)/shard_map/sub | solution.py:33
  137.7 1.0 fusion.18
  138.7 0.2 copy.102
  138.9 0.0 copy-start.3
  138.9 0.6 reshape.165
  139.6 18.1 %all_to_all.8 = bf16[2,8,32,512]{3,2,0,1:T(8,128)(2,1)S(1)} all-to-all(bf16[2,8,32,512]{3,2,0,1:T(8,128)(2,1)S(1)} %reshape.165), channel_id=1, replica_groups=mesh['fsdp'=4,'tm'=8] {'tm'}, dimensions={1} | all-to-all | bytes 1048576 | tf_op jit(solution)/shard_map/all_to_all | solution.py:82
  157.7 0.0 all-gather.11.cloned.1.call-done
  157.7 0.0 copy-done.3
  157.7 2.9 %add_convert_fusion = bf16[512,1024]{1,0:T(8,128)(2,1)} fusion(bf16[512,1024]{1,0:T(8,128)(2,1)S(1)} %copy-done.3, bf16[512,512]{1,0:T(8,128)(2,1)S(1)} %bitcast.64, bf16[512,1024]{1,0:T(8,128)(2,1)} %all-gather.11.cloned.1.call-done), kind=kOutput, calls=%fused_computation.19 | convolution fusion | flops 538443776 | bytes 3670016 | tf_op jit(solution)/shard_map/dot_general | solution.py:53
  (5 shorter events, 0.1 us)
Async XLA Ops:
  6.5 2.2 %copy-start = (bf16[2,1,256,1024]{3,2,1,0:T(8,128)(2,1)S(1)}, bf16[2,1,256,1024]{3,2,1,0:T(8,128)(2,1)}, u32[]{:S(2)}) copy-start(bf16[2,1,256,1024]{3,2,1,0:T(8,128)(2,1)} %param.7) | copy-start | bytes 3145732
  6.5 33.6 %copy-start.5 = (f32[1024]{0:T(1024)S(1)}, f32[1024]{0:T(1024)}, u32[]{:S(2)}) copy-start(f32[1024]{0:T(1024)} %param.8) | copy-start | bytes 12292
  6.5 33.6 %all-gather.5.cloned.1.call-start = ((), (), s32[]{:S(2)}) async-start(), calls=%async_computation.2 | async-start | bytes 3932160 | tf_op jit(solution)/shard_map/all_gather | solution.py:47
  7.3 54.3 %all-gather.7.cloned.1.call-start = ((), (), s32[]{:S(2)}) async-start(), calls=%async_computation.3 | async-start | bytes 1310720 | tf_op jit(solution)/shard_map/all_gather | solution.py:56
  8.0 94.2 %all-gather.9.cloned.1.call-start = ((), (), s32[]{:S(2)}) async-start(), calls=%async_computation.4 | async-start | bytes 3932160 | tf_op jit(solution)/shard_map/all_gather | solution.py:47
  44.0 1.7 %copy-start.1 = (f32[2,256,1,1536]{3,1,0,2:T(8,128)}, f32[2,256,1,1536]{3,1,0,2:T(8,128)S(1)}, u32[]{:S(2)}) copy-start(f32[2,256,1,1536]{3,1,0,2:T(8,128)S(1)} %convolution_bitcast_fusion) | copy-start | bytes 9437188
  57.2 3.3 %copy-start.4 = (bf16[2,256,1,512]{1,3,0,2:T(8,128)(2,1)S(1)}, bf16[2,256,1,512]{1,3,0,2:T(8,128)(2,1)}, u32[]{:S(2)}) copy-start(bf16[2,256,1,512]{1,3,0,2:T(8,128)(2,1)} %copy.81) | copy-start | bytes 1572868
  63.6 1.0 copy-start.2
  66.6 31.7 %all-to-all-start = ((bf16[2,1,256,1024]{3,0,1,2:T(2,128)(2,1)}), bf16[2,1,256,1024]{3,0,1,2:T(2,128)(2,1)S(1)}, u32[]{:S(2)}, u32[]{:S(2)}) async-start(bf16[2,1,256,1024]{3,0,1,2:T(2,128)(2,1)} %copy.86), calls=%async_computation | async-start | bytes 2097152 | tf_op jit(solution)/shard_map/all_to_all | solution.py:74
  72.1 85.6 %all-gather.11.cloned.1.call-start = ((), (), s32[]{:S(2)}) async-start(), calls=%async_computation.5 | async-start | bytes 1310720 | tf_op jit(solution)/shard_map/all_gather | solution.py:56
  99.0 3.2 %copy-start.6 = (f32[1024]{0:T(1024)S(1)}, f32[1024]{0:T(1024)}, u32[]{:S(2)}) copy-start(f32[1024]{0:T(1024)} %param.11) | copy-start | bytes 12292
  138.9 18.8 %copy-start.3 = (bf16[512,1024]{1,0:T(8,128)(2,1)S(1)}, bf16[512,1024]{1,0:T(8,128)(2,1)}, u32[]{:S(2)}) copy-start(bf16[512,1024]{1,0:T(8,128)(2,1)} %copy-done.2) | copy-start | bytes 3145732
Sparse Core Ops, SparseCore 0:
  8.9 31.2 all-gather.4
  41.7 16.6 all-gather.6
  60.0 28.4 all-gather.8
  90.0 16.6 all-gather.10
where the time goes:
time: 168 us; the launch traced here: 167 us
  waiting for transfers between devices  59 us (35%)
  matrix products  26.8 us (16%)
  other arithmetic  24.1 us (14%)
  local copies, waits for them, and re-layouts  20.1 us (12%)
  blocking collectives  18.1 us (11%)
  between operations  13.4 us (8%)
  starting transfers between devices  5.61 us (3%)
    all_gather x2, waiting for transfers between devices, project_inputs(): lax.all_gather(weight, 'fsdp', axis=0, tiled=True)  30.8 us
    all_to_all x1, waiting for transfers between devices, shards(): lax.all_to_all(middle, 'tm', split_axis=2, concat_axis=1, tiled=True)  25.6 us
    sub x2, other arithmetic, attention_core(): exponent = jnp.exp(scores - row_max)  19.8 us
    all_to_all x1, blocking collectives, shards(): lax.all_to_all(context_t, 'tm', split_axis=1, concat_axis=2, tiled=True)  18.1 us
    dot_general x2, matrix products, attention_core(): jnp.einsum('blmhe,bkmhe->bmhlk', queries, key_rows, precision=lax.Precisi...  12.6 us
    dot_general x2, matrix products, add_rows(): return jnp.dot(normed, segment, preferred_element_type=jnp.float32)  7.81 us
    all_to_all x1, starting transfers between devices, shards(): lax.all_to_all(middle, 'tm', split_axis=2, concat_axis=1, tiled=True)  5.5 us
    dot_general x2, matrix products, add_rows(): return jnp.dot(context, segment, preferred_element_type=jnp.float32)  4.86 us
  transfers between devices with their start and end apart: 5, of which 2 were waited for; matrix products, arithmetic and copies ran while one was open for 39% of the time, Pallas kernels for 0%

commit v1 on v0

v1 whole, which is shorter than its diff:
```python
import functools

import jax
import jax.numpy as jnp
from jax import lax
from jax.experimental import pallas as pl
from jax.experimental.pallas import tpu as pltpu
from jax.sharding import PartitionSpec as P

HEAD = 64
LANES = 128
EPSILON = 1e-06
MESH = pl.DeviceIdType.MESH
BF16 = jnp.bfloat16
F32 = jnp.float32


def pieces_of(depth):
    return max(1, depth // 64)


def kernel(
    n_f, n_t, tok, sg, sqkv, sout, tg, tqkv, tout, out,
    xv, normed, proj, ctx, mid, arrived, ctx_t, ctx_back, wsq, wso, wtq, wto, outv,
    local_sem, w_local, w_send, w_recv, m_send, m_recv, o_send, o_recv,
    a_send, a_recv, c_send, c_recv, own_sem, out_sem,
):
    f = lax.axis_index("fsdp")
    t = lax.axis_index("tm")
    mate = f + 1 - 2 * (f % 2)
    peers = n_f // 2 - 1
    clips = xv.shape[0]
    rows, width = xv.shape[1:]
    places = rows // n_t
    inner = wso.shape[0]

    barrier = pltpu.get_barrier_semaphore()
    pl.semaphore_signal(barrier, inc=1, device_id={"fsdp": mate}, device_id_type=MESH)
    for k in range(1, peers + 1):
        pl.semaphore_signal(
            barrier, inc=1, device_id={"fsdp": (f + 2 * k) % n_f}, device_id_type=MESH
        )
    for j in range(1, n_t):
        pl.semaphore_signal(
            barrier, inc=1, device_id={"tm": (t + j) % n_t}, device_id_type=MESH
        )

    token_copy = pltpu.make_async_copy(tok, xv, local_sem)
    token_copy.start()
    weights = ((sqkv, wsq), (sout, wso), (tqkv, wtq), (tout, wto))
    own_weights = []
    for w, (src, dst) in enumerate(weights):
        depth = src.shape[0]
        cp = pltpu.make_async_copy(src, dst.at[pl.ds(f * depth, depth)], w_local.at[w])
        cp.start()
        own_weights.append(cp)

    pl.semaphore_wait(barrier, 1 + peers + n_t - 1)

    sends = []

    def peer_copy(w, k, p, source):
        src, dst = weights[w]
        depth = src.shape[0]
        size = depth // pieces_of(depth)
        return pltpu.make_async_remote_copy(
            src_ref=src.at[pl.ds(p * size, size)],
            dst_ref=dst.at[pl.ds(pl.multiple_of(source * depth + p * size, size), size)],
            send_sem=w_send.at[w, k, p],
            recv_sem=w_recv.at[w, k, p],
            device_id={"fsdp": (f + 2 * (k + 1)) % n_f},
            device_id_type=MESH,
        )

    def mate_own(w, source):
        src, dst = weights[w]
        depth = src.shape[0]
        return pltpu.make_async_remote_copy(
            src_ref=src,
            dst_ref=dst.at[pl.ds(pl.multiple_of(source * depth, depth), depth)],
            send_sem=o_send.at[w],
            recv_sem=o_recv.at[w],
            device_id={"fsdp": mate},
            device_id_type=MESH,
        )

    def mate_forward(w, k, p, source):
        src, dst = weights[w]
        depth = src.shape[0]
        size = depth // pieces_of(depth)
        where = pl.ds(pl.multiple_of(source * depth + p * size, size), size)
        return pltpu.make_async_remote_copy(
            src_ref=dst.at[where],
            dst_ref=dst.at[where],
            send_sem=m_send.at[w, k, p],
            recv_sem=m_recv.at[w, k, p],
            device_id={"fsdp": mate},
            device_id_type=MESH,
        )

    for w, (src, dst) in enumerate(weights):
        for p in range(pieces_of(src.shape[0])):
            for k in range(peers):
                cp = peer_copy(w, k, p, f)
                cp.start()
                sends.append(cp)
        cp = mate_own(w, f)
        cp.start()
        sends.append(cp)

    def relay(w):
        for p in range(pieces_of(weights[w][0].shape[0])):
            for k in range(peers):
                source = (f + n_f - 2 * (k + 1)) % n_f
                peer_copy(w, k, p, source).wait_recv()
                cp = mate_forward(w, k, p, source)
                cp.start()
                sends.append(cp)

    def gathered(w):
        own_weights[w].wait()
        mate_own(w, mate).wait_recv()
        for p in range(pieces_of(weights[w][0].shape[0])):
            for k in range(peers):
                mate_forward(w, k, p, (mate + n_f - 2 * (k + 1)) % n_f).wait_recv()

    def norm(values, gain):
        centre = values - jnp.mean(values, axis=-1, keepdims=True)
        spread = jnp.mean(centre * centre, axis=-1, keepdims=True)
        return (centre * lax.rsqrt(spread + EPSILON) * gain).astype(BF16)

    def project(c, weight):
        tile = inner

        @pl.loop(0, weight.shape[1] // tile)
        def _(i):
            cols = pl.ds(pl.multiple_of(i * tile, LANES), tile)
            part = jnp.dot(normed[c], weight[:, cols], preferred_element_type=F32)
            proj[c, :, :, cols] = part.reshape(n_t, places, tile)

    def attend(c, lo, group, count, masked, store):
        size = n_t * group
        lane = lax.broadcasted_iota(jnp.int32, (1, LANES), 1)
        first = lane < HEAD

        @pl.loop(0, inner // LANES)
        def _(i):
            def read(offset):
                cols = pl.ds(pl.multiple_of(offset + i * LANES, LANES), LANES)
                return proj[c, :, lo : lo + group, cols].reshape(size, LANES)

            q = read(0) * HEAD ** (-0.5)
            k = read(inner)
            v = read(2 * inner).astype(BF16)
            kh = k.astype(BF16)
            kl = (k - kh.astype(F32)).astype(BF16)
            kk = jnp.concatenate([kh, kh], axis=1)
            parts = []
            for h in range(LANES // HEAD):
                qm = jnp.where(first == (h == 0), q, 0.0)
                qh = qm.astype(BF16)
                ql = (qm - qh.astype(F32)).astype(BF16)
                qq = jnp.concatenate([qh, ql], axis=1)
                dims = (((1,), (1,)), ((), ()))
                s = lax.dot_general(qq, kk, dims, preferred_element_type=F32)
                s = s + lax.dot_general(qh, kl, dims, preferred_element_type=F32)
                if masked:
                    r = lax.broadcasted_iota(jnp.int32, (size, size), 0)
                    l = lax.broadcasted_iota(jnp.int32, (size, size), 1)
                    s = jnp.where(lax.rem(r, group) == lax.rem(l, group), s, -1e30)
                e = jnp.exp(s - jnp.max(s, axis=-1, keepdims=True))
                total = jnp.sum(e, axis=-1, keepdims=True)
                pv = jnp.dot(e.astype(BF16), v, preferred_element_type=F32)
                parts.append(pv / total)
            result = jnp.where(first, parts[0], parts[1])
            store(pl.ds(pl.multiple_of(i * LANES, LANES), LANES), result)

    def a2a(c, j, slot_from, send):
        to = (t + j) % n_t
        return pltpu.make_async_remote_copy(
            src_ref=mid.at[c, to],
            dst_ref=arrived.at[c, slot_from],
            send_sem=a_send.at[c, j],
            recv_sem=a_recv.at[c, j],
            device_id={"tm": to},
            device_id_type=MESH,
        )

    def back(c, j, slot_from):
        to = (t + j) % n_t
        return pltpu.make_async_remote_copy(
            src_ref=ctx_t.at[c, to],
            dst_ref=ctx_back.at[c, slot_from],
            send_sem=c_send.at[c, j],
            recv_sem=c_recv.at[c, j],
            device_id={"tm": to},
            device_id_type=MESH,
        )

    token_copy.wait()
    block = min(rows, 64)
    for c in range(clips):

        @pl.loop(0, rows // block)
        def _(i):
            where = pl.ds(pl.multiple_of(i * block, block), block)
            normed[c, where] = norm(xv[c, where].astype(F32), sg[...])

    relay(0)
    gathered(0)
    for c in range(clips):
        project(c, wsq)
    own_copies = []
    for c in range(clips):

        def store_spatial(cols, result):
            ctx[:, cols] = result.astype(BF16)

        attend(c, 0, places, 1, False, store_spatial)
        if c == 0:
            relay(1)
            gathered(1)

        @pl.loop(0, width // inner)
        def _(i):
            cols = pl.ds(pl.multiple_of(i * inner, LANES), inner)
            part = xv[c, :, cols].astype(F32) + jnp.dot(
                ctx[...], wso[:, cols], preferred_element_type=F32
            )
            mid[c, :, :, cols] = part.reshape(n_t, places, inner).astype(BF16)

        for j in range(1, n_t):
            cp = a2a(c, j, t, True)
            cp.start()
            sends.append(cp)
        cp = pltpu.make_async_copy(mid.at[c, t], arrived.at[c, t], own_sem.at[0, c])
        cp.start()
        own_copies.append(cp)

    relay(2)
    own_back = []
    group = min(places, 16)
    for c in range(clips):
        own_copies[c].wait()
        for j in range(1, n_t):
            a2a(c, j, (t + n_t - j) % n_t, False).wait_recv()
        step = max(1, block // places)

        @pl.loop(0, n_t // step)
        def _(i):
            values = arrived[c, pl.ds(i * step, step)].astype(F32).reshape(step * places, width)
            where = pl.ds(pl.multiple_of(i * step * places, step * places), step * places)
            normed[c, where] = norm(values, tg[...])

        if c == 0:
            gathered(2)
        project(c, wtq)
        for g in range(places // group):

            def store_temporal(cols, result):
                ctx_t[c, :, g * group : (g + 1) * group, cols] = result.reshape(
                    n_t, group, LANES
                ).astype(BF16)

            attend(c, g * group, group, n_t, True, store_temporal)
        for j in range(1, n_t):
            cp = back(c, j, t)
            cp.start()
            sends.append(cp)
        cp = pltpu.make_async_copy(ctx_t.at[c, t], ctx_back.at[c, t], own_sem.at[1, c])
        cp.start()
        own_back.append(cp)
        if c == 0:
            relay(3)
    gathered(3)
    finals = []
    for c in range(clips):
        own_back[c].wait()
        for j in range(1, n_t):
            back(c, j, (t + n_t - j) % n_t).wait_recv()
        ctx[...] = ctx_back[c].astype(F32).reshape(rows, inner).astype(BF16)

        @pl.loop(0, width // inner)
        def _(i):
            cols = pl.ds(pl.multiple_of(i * inner, LANES), inner)
            part = mid[c, :, :, cols].astype(F32).reshape(rows, inner) + jnp.dot(
                ctx[...], wto[:, cols], preferred_element_type=F32
            )
            outv[c, :, cols] = part.astype(BF16)

        cp = pltpu.make_async_copy(outv.at[c], out.at[c], out_sem.at[c])
        cp.start()
        finals.append(cp)
    for cp in sends:
        cp.wait_send()
    for cp in finals:
        cp.wait()


def shards(
    n_f, n_t, tokens, spatial_gain, spatial_qkv, spatial_out, temporal_gain, temporal_qkv,
    temporal_out,
):
    clip_count, frames, rows, width = tokens.shape
    assert frames == 1
    inner = spatial_out.shape[0] * n_f
    columns = spatial_qkv.shape[1]
    places = rows // n_t
    peers = max(1, n_f // 2 - 1)
    most = pieces_of(max(spatial_qkv.shape[0], spatial_out.shape[0]))
    anywhere = pl.BlockSpec(memory_space=pl.ANY)
    vmem = pl.BlockSpec(memory_space=pltpu.VMEM)
    dma = pltpu.SemaphoreType.DMA
    result = pl.pallas_call(
        functools.partial(kernel, n_f, n_t),
        out_shape=jax.ShapeDtypeStruct((clip_count, rows, width), BF16),
        in_specs=[anywhere, vmem, anywhere, anywhere, vmem, anywhere, anywhere],
        out_specs=anywhere,
        scratch_shapes=[
            pltpu.VMEM((clip_count, rows, width), BF16),
            pltpu.VMEM((clip_count, rows, width), BF16),
            pltpu.VMEM((clip_count, n_t, places, columns), F32),
            pltpu.VMEM((rows, inner), BF16),
            pltpu.VMEM((clip_count, n_t, places, width), BF16),
            pltpu.VMEM((clip_count, n_t, places, width), BF16),
            pltpu.VMEM((clip_count, n_t, places, inner), BF16),
            pltpu.VMEM((clip_count, n_t, places, inner), BF16),
            pltpu.VMEM((width, columns), BF16),
            pltpu.VMEM((inner, width), BF16),
            pltpu.VMEM((width, columns), BF16),
            pltpu.VMEM((inner, width), BF16),
            pltpu.VMEM((clip_count, rows, width), BF16),
            dma,
            dma((4,)),
            dma((4, peers, most)),
            dma((4, peers, most)),
            dma((4, peers, most)),
            dma((4, peers, most)),
            dma((4,)),
            dma((4,)),
            dma((clip_count, n_t)),
            dma((clip_count, n_t)),
            dma((clip_count, n_t)),
            dma((clip_count, n_t)),
            dma((2, clip_count)),
            dma((clip_count,)),
        ],
        compiler_params=pltpu.CompilerParams(
            collective_id=0, has_side_effects=True, vmem_limit_bytes=50 * 1024 * 1024
        ),
    )(
        tokens.reshape(clip_count, rows, width),
        spatial_gain.reshape(1, width),
        spatial_qkv,
        spatial_out,
        temporal_gain.reshape(1, width),
        temporal_qkv,
        temporal_out,
    )
    return result.reshape(clip_count, frames, rows, width)


def solution(mesh):
    placed = (
        P("fsdp", "tm", None, None),
        P(),
        P("fsdp", None),
        P("fsdp", None),
        P(),
        P("fsdp", None),
        P("fsdp", None),
    )
    body = functools.partial(shards, mesh.shape["fsdp"], mesh.shape["tm"])
    return jax.shard_map(
        body, mesh=mesh, in_specs=placed, out_specs=P("fsdp", "tm", None, None), check_vma=False
    )
```

time: 168 us -> 82.6 us (0.49)
  Pallas kernels: 0 us -> 75.8 us
  waiting for transfers between devices: 59 us -> 0 us
  matrix products: 26.8 us -> 0 us
  other arithmetic: 24.1 us -> 0 us
  blocking collectives: 18.1 us -> 0 us
  local copies, waits for them, and re-layouts: 20.1 us -> 6.51 us
  between operations: 13.4 us -> 0.02 us
  starting transfers between devices: 5.61 us -> 0 us
    pallas_call x0 -> x1, Pallas kernels: none -> 75.8 us  [shards(): pl.pallas_call(functools.partial(kernel, n_f, n_t), out_shape=jax.ShapeDt...]
    all_gather x4 -> x0, waiting for transfers between devices: 30.8 us -> none  [the longest x2 30.8 us: project_inputs(): lax.all_gather(weight, 'fsdp', axis=0, tiled=True)]
    dot_general x8 -> x0, matrix products: 26.8 us -> none  [the longest x2 12.6 us: attention_core(): jnp.einsum('blmhe,bkmhe->bmhlk', queries, key_rows, precision=lax.Precisi...]
    all_to_all x1 -> x0, waiting for transfers between devices: 25.6 us -> none  [shards(): lax.all_to_all(middle, 'tm', split_axis=2, concat_axis=1, tiled=True)]
    sub x2 -> x0, other arithmetic: 19.8 us -> none  [attention_core(): exponent = jnp.exp(scores - row_max)]
    all_to_all x1 -> x0, blocking collectives: 18.1 us -> none  [shards(): lax.all_to_all(context_t, 'tm', split_axis=1, concat_axis=2, tiled=True)]
    slice x7 -> x0, local copies, waits for them, and re-layouts: 8.76 us -> none  [the longest x2 4.15 us: attention_core(): projected[..., inner_width:2 * inner_width]]
    reshape x6 -> x0, local copies, waits for them, and re-layouts: 7.83 us -> none  [the longest x1 2.04 us: shards(): middle = middle.reshape(clip_count, frames, places, feature_width)]
  transfers between devices with their start and end apart: 5 -> 0, of which waited for: 2 -> 0; matrix products, arithmetic and copies ran while one was open for 39% -> 0% of each run, Pallas kernels for 0% -> 0%
where the time goes in v1:
time: 82.6 us; the launch traced here: 82.3 us
  Pallas kernels  75.8 us (92%)
  local copies, waits for them, and re-layouts  6.51 us (8%)
    pallas_call x1, Pallas kernels, shards(): pl.pallas_call(functools.partial(kernel, n_f, n_t), out_shape=jax.ShapeDt...  75.8 us
    unnamed x13, local copies, waits for them, and re-layouts  6.51 us

profile of v1, /device:TPU:0, one launch (start us, length us, event | category | flops | bytes accessed | tf_op | source)
XLA Modules:
  0.0 82.3 jit_solution(13152402072178094240)
XLA Ops:
  0.0 0.0 copy-start.4
  0.0 0.7 copy-done.4
  0.7 0.0 copy-start
  0.7 1.1 %copy-done = bf16[256,1536]{1,0:T(8,128)(2,1)S(1)} copy-done((bf16[256,1536]{1,0:T(8,128)(2,1)S(1)}, bf16[256,1536]{1,0:T(8,128)(2,1)}, u32[]{:S(2)}) %copy-start) | copy-done | bytes 786456
  1.8 0.0 copy-start.1
  1.8 1.1 %copy-done.1 = bf16[256,1536]{1,0:T(8,128)(2,1)S(1)} copy-done((bf16[256,1536]{1,0:T(8,128)(2,1)S(1)}, bf16[256,1536]{1,0:T(8,128)(2,1)}, u32[]{:S(2)}) %copy-start.1) | copy-done | bytes 786456
  3.0 0.0 copy-start.2
  3.0 0.9 %copy-done.2 = bf16[128,1024]{1,0:T(8,128)(2,1)S(1)} copy-done((bf16[128,1024]{1,0:T(8,128)(2,1)S(1)}, bf16[128,1024]{1,0:T(8,128)(2,1)}, u32[]{:S(2)}) %copy-start.2) | copy-done | bytes 262168
  3.9 0.0 copy-start.3
  3.9 0.9 %copy-done.3 = bf16[128,1024]{1,0:T(8,128)(2,1)S(1)} copy-done((bf16[128,1024]{1,0:T(8,128)(2,1)S(1)}, bf16[128,1024]{1,0:T(8,128)(2,1)}, u32[]{:S(2)}) %copy-start.3) | copy-done | bytes 262168
  4.9 0.0 copy-start.5
  4.9 0.7 copy-done.5
  5.5 75.8 %shard_map.73 = bf16[2,256,1024]{2,1,0:T(8,128)(2,1)S(1)} custom-call(bf16[2,256,1024]{2,1,0:T(8,128)(2,1)} %bitcast.9, f32[1,1024]{1,0:T(1,128)S(1)} %bitcast.7, bf16[256,1536]{1,0:T(8,128)(2,1)S(1)} %copy-done, bf16[128,1024]{1,0:T(8,128)(2,1)S(1)} %copy-done.2, f32[1,1024]{1,0:T(1,128)S(1)} %bitcast.8, bf16[256,1536]{1,0:T(8,128)(2,1)S(1)} %copy-done.1, ...), custom_call_target="tpu_custom_call" | custom-call | tf_op jit(solution)/shard_map/pallas_call | solution.py:314
  81.3 1.0 %copy.10 = bf16[2,1,256,1024]{3,2,1,0:T(8,128)(2,1)} copy(bf16[2,1,256,1024]{3,2,1,0:T(8,128)(2,1)S(1)} %bitcast.6) | data formatting | bytes 2097152
Async XLA Ops:
  0.0 0.7 copy-start.4
  0.7 1.1 %copy-start = (bf16[256,1536]{1,0:T(8,128)(2,1)S(1)}, bf16[256,1536]{1,0:T(8,128)(2,1)}, u32[]{:S(2)}) copy-start(bf16[256,1536]{1,0:T(8,128)(2,1)} %sqkv.1) | copy-start | bytes 2359300
  1.8 1.1 %copy-start.1 = (bf16[256,1536]{1,0:T(8,128)(2,1)S(1)}, bf16[256,1536]{1,0:T(8,128)(2,1)}, u32[]{:S(2)}) copy-start(bf16[256,1536]{1,0:T(8,128)(2,1)} %tqkv.1) | copy-start | bytes 2359300
  3.0 0.9 %copy-start.2 = (bf16[128,1024]{1,0:T(8,128)(2,1)S(1)}, bf16[128,1024]{1,0:T(8,128)(2,1)}, u32[]{:S(2)}) copy-start(bf16[128,1024]{1,0:T(8,128)(2,1)} %sout.1) | copy-start | bytes 786436
  3.9 0.9 %copy-start.3 = (bf16[128,1024]{1,0:T(8,128)(2,1)S(1)}, bf16[128,1024]{1,0:T(8,128)(2,1)}, u32[]{:S(2)}) copy-start(bf16[128,1024]{1,0:T(8,128)(2,1)} %tout.1) | copy-start | bytes 786436
  4.9 0.7 copy-start.5

commit v2 on v1

--- a/solution.py
+++ b/solution.py
@@ -16,7 +16,7 @@
 
 
 def pieces_of(depth):
-    return max(1, depth // 64)
+    return max(2, depth // 32)
 
 
 def kernel(
@@ -98,10 +98,79 @@
             device_id_type=MESH,
         )
 
+    parity = t % 2
+    partner = t + 1 - 2 * parity
+    half = pieces_of(sqkv.shape[0]) // 2
+    small = sqkv.shape[0] // pieces_of(sqkv.shape[0])
+
+    def half_rows(source, part, i):
+        start = source * sqkv.shape[0] + (part * half + i) * small
+        return pl.ds(pl.multiple_of(start, small), small)
+
+    def direct(k, i, source):
+        return pltpu.make_async_remote_copy(
+            src_ref=sqkv.at[pl.ds(pl.multiple_of((parity * half + i) * small, small), small)],
+            dst_ref=wsq.at[half_rows(source, parity, i)],
+            send_sem=w_send.at[0, k, i],
+            recv_sem=w_recv.at[0, k, i],
+            device_id={"fsdp": (f + 2 * (k + 1)) % n_f},
+            device_id_type=MESH,
+        )
+
+    def cross(k, i, source, part):
+        return pltpu.make_async_remote_copy(
+            src_ref=wsq.at[half_rows(source, part, i)],
+            dst_ref=wsq.at[half_rows(source, part, i)],
+            send_sem=w_send.at[0, k, half + i],
+            recv_sem=w_recv.at[0, k, half + i],
+            device_id={"tm": partner},
+            device_id_type=MESH,
+        )
+
+    def half_forward(k, i, source, part, slot):
+        return pltpu.make_async_remote_copy(
+            src_ref=wsq.at[half_rows(source, part, i)],
+            dst_ref=wsq.at[half_rows(source, part, i)],
+            send_sem=m_send.at[0, k, slot],
+            recv_sem=m_recv.at[0, k, slot],
+            device_id={"fsdp": mate},
+            device_id_type=MESH,
+        )
+
+    def source_of(who, k):
+        return (who + n_f - 2 * (k + 1)) % n_f
+
+    def relay_first():
+        for i in range(half + 1):
+            for k in range(peers):
+                source = source_of(f, k)
+                if i < half:
+                    direct(k, i, source).wait_recv()
+                    for cp in (
+                        cross(k, i, source, parity),
+                        half_forward(k, i, source, parity, i),
+                    ):
+                        cp.start()
+                        sends.append(cp)
+                if i > 0:
+                    cross(k, i - 1, source, 1 - parity).wait_recv()
+                    cp = half_forward(k, i - 1, source, 1 - parity, half + i - 1)
+                    cp.start()
+                    sends.append(cp)
+
+    def gathered_first():
+        own_weights[0].wait()
+        mate_own(0, mate).wait_recv()
+        for i in range(half):
+            for k in range(peers):
+                source = source_of(mate, k)
+                half_forward(k, i, source, parity, i).wait_recv()
+                half_forward(k, i, source, 1 - parity, half + i).wait_recv()
+
     for w, (src, dst) in enumerate(weights):
-        for p in range(pieces_of(src.shape[0])):
+        for p in range(half if w == 0 else pieces_of(src.shape[0])):
             for k in range(peers):
-                cp = peer_copy(w, k, p, f)
+                cp = direct(k, p, f) if w == 0 else peer_copy(w, k, p, f)
                 cp.start()
                 sends.append(cp)
         cp = mate_own(w, f)
@@ -206,8 +275,8 @@
             where = pl.ds(pl.multiple_of(i * block, block), block)
             normed[c, where] = norm(xv[c, where].astype(F32), sg[...])
 
-    relay(0)
-    gathered(0)
+    relay_first()
+    gathered_first()
     for c in range(clips):
         project(c, wsq)
     own_copies = []
@@ -346,7 +415,7 @@
             dma((clip_count,)),
         ],
         compiler_params=pltpu.CompilerParams(
-            collective_id=0, has_side_effects=True, vmem_limit_bytes=50 * 1024 * 1024
+            collective_id=0, has_side_effects=True, vmem_limit_bytes=67000000
         ),
     )(
         tokens.reshape(clip_count, rows, width),

time: 82.6 us -> 75.4 us (0.913)
  local copies, waits for them, and re-layouts: 6.51 us -> 2.26 us
  Pallas kernels: 75.8 us -> 72.9 us
    unnamed x13 -> x1, local copies, waits for them, and re-layouts: 6.51 us -> 2.26 us
    pallas_call x1, Pallas kernels: 75.8 us -> 72.9 us  [shards(): pl.pallas_call(functools.partial(kernel, n_f, n_t), out_shape=jax.ShapeDt...]
where the time goes in v2:
time: 75.4 us; the launch traced here: 75.2 us
  Pallas kernels  72.9 us (97%)
  local copies, waits for them, and re-layouts  2.26 us (3%)
    pallas_call x1, Pallas kernels, shards(): pl.pallas_call(functools.partial(kernel, n_f, n_t), out_shape=jax.ShapeDt...  72.9 us
    unnamed x1, local copies, waits for them, and re-layouts  2.26 us

profile of v2, /device:TPU:0, one launch (start us, length us, event | category | flops | bytes accessed | tf_op | source)
XLA Modules:
  0.0 75.2 jit_solution(256542759629622715)
XLA Ops:
  0.0 72.9 %shard_map.73 = bf16[2,256,1024]{2,1,0:T(8,128)(2,1)} custom-call(bf16[2,256,1024]{2,1,0:T(8,128)(2,1)} %bitcast.7, f32[1,1024]{1,0:T(1,128)} %bitcast.8, bf16[256,1536]{1,0:T(8,128)(2,1)} %sqkv.1, bf16[128,1024]{1,0:T(8,128)(2,1)} %sout.1, f32[1,1024]{1,0:T(1,128)} %bitcast.9, bf16[256,1536]{1,0:T(8,128)(2,1)} %tqkv.1, bf16[128,1024]{1,0:T(8,128)(2,1)} %tout.1), custom_call_target="tpu_custom_call" | custom-call | tf_op jit(solution)/shard_map/pallas_call | solution.py:383
  72.9 2.3 %copy.10 = bf16[2,1,256,1024]{3,2,1,0:T(8,128)(2,1)} copy(bf16[2,1,256,1024]{3,2,1,0:T(8,128)(2,1)} %bitcast.6) | data formatting | bytes 2097152

commit v3 on v2

--- a/solution.py
+++ b/solution.py
@@ -212,7 +212,12 @@
         lane = lax.broadcasted_iota(jnp.int32, (1, LANES), 1)
         first = lane < HEAD
 
-        @pl.loop(0, inner // LANES)
+        if masked:
+            r = lax.rem(lax.broadcasted_iota(jnp.int32, (size, 1), 0), group)
+            l = lax.rem(lax.broadcasted_iota(jnp.int32, (1, size), 1), group)
+            same_place = r == l
+
+        @pl.loop(0, inner // LANES, unroll=2)
         def _(i):
             def read(offset):
                 cols = pl.ds(pl.multiple_of(offset + i * LANES, LANES), LANES)
@@ -234,9 +239,7 @@
                 s = lax.dot_general(qq, kk, dims, preferred_element_type=F32)
                 s = s + lax.dot_general(qh, kl, dims, preferred_element_type=F32)
                 if masked:
-                    r = lax.broadcasted_iota(jnp.int32, (size, size), 0)
-                    l = lax.broadcasted_iota(jnp.int32, (size, size), 1)
-                    s = jnp.where(lax.rem(r, group) == lax.rem(l, group), s, -1e30)
+                    s = jnp.where(same_place, s, -1e30)
                 e = jnp.exp(s - jnp.max(s, axis=-1, keepdims=True))
                 total = jnp.sum(e, axis=-1, keepdims=True)
                 pv = jnp.dot(e.astype(BF16), v, preferred_element_type=F32)

time: 75.4 us -> 74.7 us (level)
  no operation moved by 1% of the time
where the time goes in v3:
time: 74.7 us; the launch traced here: 74.5 us
  Pallas kernels  72.3 us (97%)
  local copies, waits for them, and re-layouts  2.26 us (3%)
    pallas_call x1, Pallas kernels, shards(): pl.pallas_call(functools.partial(kernel, n_f, n_t), out_shape=jax.ShapeDt...  72.3 us
    unnamed x1, local copies, waits for them, and re-layouts  2.26 us

profile of v3, /device:TPU:0, one launch (start us, length us, event | category | flops | bytes accessed | tf_op | source)
XLA Modules:
  0.0 74.5 jit_solution(14066856075550617031)
XLA Ops:
  0.0 72.3 %shard_map.73 = bf16[2,256,1024]{2,1,0:T(8,128)(2,1)} custom-call(bf16[2,256,1024]{2,1,0:T(8,128)(2,1)} %bitcast.7, f32[1,1024]{1,0:T(1,128)} %bitcast.8, bf16[256,1536]{1,0:T(8,128)(2,1)} %sqkv.1, bf16[128,1024]{1,0:T(8,128)(2,1)} %sout.1, f32[1,1024]{1,0:T(1,128)} %bitcast.9, bf16[256,1536]{1,0:T(8,128)(2,1)} %tqkv.1, bf16[128,1024]{1,0:T(8,128)(2,1)} %tout.1), custom_call_target="tpu_custom_call" | custom-call | tf_op jit(solution)/shard_map/pallas_call | solution.py:386
  72.3 2.3 %copy.10 = bf16[2,1,256,1024]{3,2,1,0:T(8,128)(2,1)} copy(bf16[2,1,256,1024]{3,2,1,0:T(8,128)(2,1)} %bitcast.6) | data formatting | bytes 2097152
